TPU v7x, 32 devices: a whole 2x2x4 slice. The times are simulated.
32 devices in a mesh: bits: 16 (over z, y, x), docs: 2 (over core).
Axes of the slice: x: 2, y: 2, z: 4, core: 2. Of those that a mesh axis runs over, the one named last changes fastest.
Arguments:
- positions: int32 [1024, 4096], P(('bits', 'docs')), may hold values from 0 to 4095
- element_weights: float32 [1024, 1024], P(('bits', 'docs')), may hold values from 0.25 to 4
- set_sizes: int32 [1024], P(('bits', 'docs')), may hold values from 256 to 1024, as said below
- bit_weights: bfloat16 [4096], replicated, may hold values from 0.25 to 4
- candidates: int32 [2, 16, 16], P('docs'), may hold values from 0 to 63, as said below
Outputs:
- scores: float32 [2, 16, 128, 64], P('docs', 'bits')
Inputs may be any that keep to these rules, and one draw needn't show every extreme that they name: `set_sizes`: one document in every draw has exactly 1024 elements. `candidates`: the 16 row tiles named for one block are distinct. `positions`: entries of a row beyond its first 4 * set_sizes are not part of the filter.
All inputs are finite; a program needn't handle non-finite values.
Results may differ from a plain program's by a relative error of at most 0.0012.
Values may be sent and summed in bfloat16 or wider, within the bound.
A program may use at most 64 MiB of HBM per device.

v0:
```python
import math
import jax
import jax.numpy as jnp
from jax import lax
from jax.sharding import PartitionSpec as P

FILTER_BITS = 4096
HASHES = 4
TILE = 8


def build_filter(positions, element_weights, set_sizes):
    doc_count, slot_count = positions.shape
    elem_count = element_weights.shape[1]
    low_cells = 64
    high_cells = FILTER_BITS // low_cells
    slot_index = jnp.arange(slot_count, dtype=jnp.int32)
    usable = slot_index[None, :] < HASHES * set_sizes[:, None]
    spread = jnp.broadcast_to(element_weights[:, :, None], (doc_count, elem_count, HASHES)).reshape(
        doc_count, slot_count
    )
    slot_weights = jnp.where(usable, spread, 0.0)
    upper = slot_weights.astype(jnp.bfloat16)
    remain = slot_weights - upper.astype(jnp.float32)
    middle = remain.astype(jnp.bfloat16)
    lower = (remain - middle.astype(jnp.float32)).astype(jnp.bfloat16)
    weight_parts = jnp.stack([upper, middle, lower], axis=1)
    high_index = positions // low_cells
    low_index = positions - high_index * low_cells
    group = math.gcd(doc_count, 8)

    def one_group(inputs):
        part_block, high_block, low_block = inputs
        high_onehot = (high_block[:, :, None] == jnp.arange(high_cells, dtype=jnp.int32)).astype(
            jnp.bfloat16
        )
        low_onehot = (low_block[:, :, None] == jnp.arange(low_cells, dtype=jnp.int32)).astype(
            jnp.bfloat16
        )
        left = part_block[:, :, :, None] * high_onehot[:, None, :, :]
        summed = jnp.einsum("dcph,dpl->dhl", left, low_onehot, preferred_element_type=jnp.float32)
        return summed.reshape(group, FILTER_BITS)

    grouped = lax.map(
        one_group,
        (
            weight_parts.reshape(doc_count // group, group, 3, slot_count),
            high_index.reshape(doc_count // group, group, slot_count),
            low_index.reshape(doc_count // group, group, slot_count),
        ),
    )
    return grouped.reshape(doc_count, FILTER_BITS).astype(jnp.bfloat16)


def weighted_pop(cells, weights):
    weighted = cells * weights
    return jnp.sum(weighted.astype(jnp.float32) * cells.astype(jnp.float32), axis=1)


def estimate(shared, pop_rows, pop_cols, size_rows, size_cols):
    union_weight = pop_rows[:, None] + pop_cols[None, :] - shared
    ratio = shared / union_weight
    smaller = jnp.minimum(size_rows[:, None], size_cols[None, :])
    return ratio * (size_rows[:, None] + size_cols[None, :]) / ((1.0 + ratio) * smaller)


def pick_tiles(slice_cells, tile_choice, row_group, groups, row_half):
    width = slice_cells.shape[1]
    row_tiles = row_half // TILE
    tiles = slice_cells.reshape(groups, row_tiles, TILE * width)
    own_tiles = lax.dynamic_index_in_dim(tiles, row_group, 0, keepdims=False)
    onehot = (tile_choice[:, :, None] == jnp.arange(row_tiles, dtype=jnp.int32)).astype(
        jnp.bfloat16
    )
    picked = jnp.einsum("jcr,rw->jcw", onehot, own_tiles, preferred_element_type=jnp.float32)
    return picked.astype(jnp.bfloat16).reshape(
        tile_choice.shape[0], tile_choice.shape[1] * TILE, width
    )


def body(positions, element_weights, set_sizes, bit_weights, candidates):
    col_index = lax.axis_index("bits")
    row_group = lax.axis_index("docs")
    blocks = lax.axis_size("bits")
    groups = lax.axis_size("docs")
    doc_total = positions.shape[0] * blocks * groups
    row_half = doc_total // groups
    col_width = doc_total // blocks
    slot_count = candidates.shape[2] * TILE
    tile_offsets = jnp.arange(TILE, dtype=jnp.int32)
    own_cells = build_filter(positions, element_weights, set_sizes)
    local_pop = weighted_pop(own_cells, bit_weights)
    every_pop, size_float = (
        lax.all_gather(local_pop, ("bits", "docs"), axis=0, tiled=True),
        lax.all_gather(set_sizes.astype(jnp.float32), ("bits", "docs"), axis=0, tiled=True),
    )
    pair_cells = lax.all_gather(own_cells, "docs", axis=0, tiled=True)
    slice_cells = lax.all_to_all(pair_cells, "bits", split_axis=1, concat_axis=0, tiled=True)
    tile_rows = row_group * row_half + (candidates[0][:, :, None] * TILE + tile_offsets).reshape(
        blocks, slot_count
    )
    picked_cells = pick_tiles(slice_cells, candidates[0], row_group, groups, row_half)
    row_cells = lax.all_to_all(picked_cells, "bits", split_axis=0, concat_axis=2, tiled=True)[0]
    shared = lax.dot_general(
        row_cells * bit_weights,
        pair_cells,
        (((1,), (1,)), ((), ())),
        preferred_element_type=jnp.float32,
    )
    row_docs = lax.dynamic_index_in_dim(tile_rows, col_index, 0, keepdims=False)
    pop_rows = every_pop[row_docs]
    pop_cols = lax.dynamic_slice_in_dim(every_pop, col_index * col_width, col_width, 0)
    size_rows = size_float[row_docs]
    size_cols = lax.dynamic_slice_in_dim(size_float, col_index * col_width, col_width, 0)
    scores = estimate(shared, pop_rows, pop_cols, size_rows, size_cols)
    return scores.reshape(1, 1, slot_count, col_width)


def solution(mesh):
    return jax.shard_map(
        body,
        mesh=mesh,
        in_specs=(
            P(("bits", "docs"), None),
            P(("bits", "docs"), None),
            P(("bits", "docs")),
            P(),
            P("docs", None, None),
        ),
        out_specs=P("docs", "bits", None, None),
        check_vma=False,
    )
```

profile of v0, /device:TPU:0, one launch (start us, length us, event | category | flops | bytes accessed | tf_op | source)
XLA Modules:
  0.0 158.0 jit_solution(18137033540736739117)
XLA Ops:
  0.0 1.1 copy.33
  1.1 0.4 broadcast_in_dim.12
  1.5 5.7 %reshape.175 = f32[4,8,1,4096]{1,0,3,2:T(4,128)} reshape(f32[32,1024,4]{0,2,1:T(4,128)S(1)} %broadcast_in_dim.12) | data formatting | bytes 1048576 | tf_op jit(solution)/shard_map/reshape | solution.py:19
  7.2 6.7 %copy.34 = f32[4,8,1,4096]{3,1,2,0:T(8,128)S(1)} copy(f32[4,8,1,4096]{1,0,3,2:T(4,128)} %reshape.175) | data formatting | bytes 1048576 | tf_op jit(solution)/shard_map/reshape | solution.py:19
  14.0 0.2 fusion.7
  14.1 0.1 fusion.6
  14.3 0.3 subtract_bitcast_fusion
  14.6 0.1 pad_maximum_fusion
  14.7 60.3 %while.10 = (s32[]{:T(128)}, bf16[4,8,4096]{2,1,0:T(8,128)(2,1)S(1)}, bf16[4,8,3,4096]{3,1,2,0:T(8,128)(2,1)S(1)}, s32[4,8,4096]{2,1,0:T(8,128)S(1)}, s32[4,8,4096]{2,1,0:T(8,128)S(1)}, /*index=5*/s32[]{:T(128)}) while((s32[]{:T(128)}, bf16[4,8,4096]{2,1,0:T(8,128)(2,1)S(1)}, bf16[4,8,3,4096]{3,1,2,0:T(8,128)(2,1)S(1)}, ...), condition=%wide.region_2.3_spmd, body=%wide.region_0.2_spmd.sunk | while | flops 304087040 | bytes 18874448 | solution.py:44
  14.8 3.0 %fusion.23 = bf16[8,4096,64]{1,2,0:T(8,128)(2,1)} fusion(s32[8,4096]{1,0:T(8,128)S(1)} %get-tuple-element.109), kind=kLoop, calls=%fused_computation.5.clone.1 | loop fusion | flops 4194304 | bytes 4325376 | tf_op jit(solution)/shard_map/while/body/eval_jaxpr/convert_element_type | solution.py:34
  17.8 0.2 copy.46
  18.0 7.9 %convert_reduce_fusion.2 = bf16[8,4096,64]{1,2,0:T(8,128)(2,1)} fusion(bf16[8,4096,64]{1,2,0:T(8,128)(2,1)} %fusion.23, bf16[8,3,4096]{2,1,0:T(4,128)(2,1)S(1)} %bitcast.50), kind=kLoop, calls=%fused_computation.2.clone.1 | loop fusion | flops 29360128 | bytes 8585216 | tf_op jit(solution)/shard_map/while/body/eval_jaxpr/dcph,dpl->dhl/reduce_sum | solution.py:41
  25.9 3.7 %fusion.24 = bf16[8,64,64]{2,1,0:T(8,128)(2,1)S(1)} fusion(bf16[8,4096,64]{1,2,0:T(8,128)(2,1)} %convert_reduce_fusion.2, s32[8,4096]{1,0:T(8,128)S(1)} %get-tuple-element.110), kind=kOutput, calls=%fused_computation.6.clone.1 | convolution fusion | flops 270532608 | bytes 4390912 | tf_op jit(solution)/shard_map/while/body/eval_jaxpr/dcph,dpl->dhl/dot_general | solution.py:41
  29.6 0.2 broadcast_in_dim.31
  29.8 3.0 %fusion.23 = bf16[8,4096,64]{1,2,0:T(8,128)(2,1)} fusion(s32[8,4096]{1,0:T(8,128)S(1)} %get-tuple-element.109), kind=kLoop, calls=%fused_computation.5.clone.1 | loop fusion | flops 4194304 | bytes 4325376 | tf_op jit(solution)/shard_map/while/body/eval_jaxpr/convert_element_type | solution.py:34
  32.9 0.2 copy.46
  33.1 7.9 %convert_reduce_fusion.2 = bf16[8,4096,64]{1,2,0:T(8,128)(2,1)} fusion(bf16[8,4096,64]{1,2,0:T(8,128)(2,1)} %fusion.23, bf16[8,3,4096]{2,1,0:T(4,128)(2,1)S(1)} %bitcast.50), kind=kLoop, calls=%fused_computation.2.clone.1 | loop fusion | flops 29360128 | bytes 8585216 | tf_op jit(solution)/shard_map/while/body/eval_jaxpr/dcph,dpl->dhl/reduce_sum | solution.py:41
  40.9 3.7 %fusion.24 = bf16[8,64,64]{2,1,0:T(8,128)(2,1)S(1)} fusion(bf16[8,4096,64]{1,2,0:T(8,128)(2,1)} %convert_reduce_fusion.2, s32[8,4096]{1,0:T(8,128)S(1)} %get-tuple-element.110), kind=kOutput, calls=%fused_computation.6.clone.1 | convolution fusion | flops 270532608 | bytes 4390912 | tf_op jit(solution)/shard_map/while/body/eval_jaxpr/dcph,dpl->dhl/dot_general | solution.py:41
  44.6 0.2 broadcast_in_dim.31
  44.9 3.0 %fusion.23 = bf16[8,4096,64]{1,2,0:T(8,128)(2,1)} fusion(s32[8,4096]{1,0:T(8,128)S(1)} %get-tuple-element.109), kind=kLoop, calls=%fused_computation.5.clone.1 | loop fusion | flops 4194304 | bytes 4325376 | tf_op jit(solution)/shard_map/while/body/eval_jaxpr/convert_element_type | solution.py:34
  48.0 0.2 copy.46
  48.1 7.9 %convert_reduce_fusion.2 = bf16[8,4096,64]{1,2,0:T(8,128)(2,1)} fusion(bf16[8,4096,64]{1,2,0:T(8,128)(2,1)} %fusion.23, bf16[8,3,4096]{2,1,0:T(4,128)(2,1)S(1)} %bitcast.50), kind=kLoop, calls=%fused_computation.2.clone.1 | loop fusion | flops 29360128 | bytes 8585216 | tf_op jit(solution)/shard_map/while/body/eval_jaxpr/dcph,dpl->dhl/reduce_sum | solution.py:41
  56.0 3.7 %fusion.24 = bf16[8,64,64]{2,1,0:T(8,128)(2,1)S(1)} fusion(bf16[8,4096,64]{1,2,0:T(8,128)(2,1)} %convert_reduce_fusion.2, s32[8,4096]{1,0:T(8,128)S(1)} %get-tuple-element.110), kind=kOutput, calls=%fused_computation.6.clone.1 | convolution fusion | flops 270532608 | bytes 4390912 | tf_op jit(solution)/shard_map/while/body/eval_jaxpr/dcph,dpl->dhl/dot_general | solution.py:41
  59.7 0.2 broadcast_in_dim.31
  60.0 3.0 %fusion.23 = bf16[8,4096,64]{1,2,0:T(8,128)(2,1)} fusion(s32[8,4096]{1,0:T(8,128)S(1)} %get-tuple-element.109), kind=kLoop, calls=%fused_computation.5.clone.1 | loop fusion | flops 4194304 | bytes 4325376 | tf_op jit(solution)/shard_map/while/body/eval_jaxpr/convert_element_type | solution.py:34
  63.0 0.2 copy.46
  63.2 7.9 %convert_reduce_fusion.2 = bf16[8,4096,64]{1,2,0:T(8,128)(2,1)} fusion(bf16[8,4096,64]{1,2,0:T(8,128)(2,1)} %fusion.23, bf16[8,3,4096]{2,1,0:T(4,128)(2,1)S(1)} %bitcast.50), kind=kLoop, calls=%fused_computation.2.clone.1 | loop fusion | flops 29360128 | bytes 8585216 | tf_op jit(solution)/shard_map/while/body/eval_jaxpr/dcph,dpl->dhl/reduce_sum | solution.py:41
  71.1 3.7 %fusion.24 = bf16[8,64,64]{2,1,0:T(8,128)(2,1)S(1)} fusion(bf16[8,4096,64]{1,2,0:T(8,128)(2,1)} %convert_reduce_fusion.2, s32[8,4096]{1,0:T(8,128)S(1)} %get-tuple-element.110), kind=kOutput, calls=%fused_computation.6.clone.1 | convolution fusion | flops 270532608 | bytes 4390912 | tf_op jit(solution)/shard_map/while/body/eval_jaxpr/dcph,dpl->dhl/dot_general | solution.py:41
  74.8 0.2 broadcast_in_dim.31
  75.0 2.3 %all_gather.9 = bf16[64,4096]{1,0:T(8,128)(2,1)S(1)} all-gather(bf16[32,4096]{1,0:T(8,128)(2,1)S(1)} %bitcast.53), channel_id=1, replica_groups=mesh['bits'=16,'docs'=2] {'docs'}, dimensions={0}, use_global_device_ids=true | all-gather | bytes 786432 | tf_op jit(solution)/shard_map/all_gather | solution.py:97
  77.3 0.8 copy.44
  78.1 8.3 %all-to-all-start = ((bf16[64,16,256]{2,0,1:T(8,128)(2,1)}), bf16[64,16,256]{2,0,1:T(8,128)(2,1)S(1)}, u32[]{:S(2)}, u32[]{:S(2)}) async-start(bf16[64,16,256]{2,0,1:T(8,128)(2,1)} %bitcast.43), calls=%async_computation | async-start | bytes 1048576 | tf_op jit(solution)/shard_map/all_to_all | solution.py:98
  86.4 15.4 %all-to-all-done = bf16[64,16,256]{2,0,1:T(8,128)(2,1)S(1)} async-done(((bf16[64,16,256]{2,0,1:T(8,128)(2,1)}), bf16[64,16,256]{2,0,1:T(8,128)(2,1)S(1)}, u32[]{:S(2)}, u32[]{:S(2)}) %all-to-all-start) | async-done | bytes 524320 | tf_op jit(solution)/shard_map/all_to_all | solution.py:98
  101.8 0.2 reshape.178
  102.0 0.5 convolution_convert_fusion
  102.5 0.5 reshape.179
  103.1 1.3 copy.37
  104.4 3.9 %all-to-all-start.1 = ((bf16[16,128,256]{1,2,0:T(8,128)(2,1)}), bf16[16,128,256]{1,2,0:T(8,128)(2,1)S(1)}, u32[]{:S(2)}, u32[]{:S(2)}) async-start(bf16[16,128,256]{1,2,0:T(8,128)(2,1)} %copy.37), calls=%async_computation.1 | async-start | bytes 2097152 | tf_op jit(solution)/shard_map/all_to_all | solution.py:103
  108.3 0.2 multiply_reduce_fusion
  108.6 0.2 dynamic-update-slice
  108.8 0.1 convert_dynamic-update-slice_fusion
  108.9 44.8 %all-reduce.2 = (f32[1024]{0:T(1024)S(1)}, f32[1024]{0:T(1024)S(1)}) all-reduce(f32[1024]{0:T(1024)S(1)} %convert_dynamic-update-slice_fusion, f32[1024]{0:T(1024)S(1)} %dynamic-update-slice), channel_id=1, replica_groups=mesh['bits'=16,'docs'=2] {'bits','docs'}, use_global_device_ids=true, to_apply=%add.1 | all-reduce | flops 2048 | bytes 16384
  153.9 0.1 add.90
  154.0 0.2 fusion.12
  154.2 1.0 gather_fusion
  155.2 1.0 gather_fusion.1
  156.2 0.8 bitcast_multiply_fusion
  157.0 1.0 divide_bitcast_fusion
  (35 shorter events, 0.6 us)
Async XLA Ops:
  7.2 6.7 %copy-start.3 = (s32[32]{0:T(128)S(1)}, s32[32]{0:T(128)}, u32[]{:S(2)}) copy-start(s32[32]{0:T(128)} %param.9) | copy-start | bytes 388
  7.2 7.1 %copy-start = (s32[32,4096]{1,0:T(8,128)S(1)}, s32[32,4096]{1,0:T(8,128)}, u32[]{:S(2)}) copy-start(s32[32,4096]{1,0:T(8,128)} %param.7) | copy-start | bytes 1572868
  14.7 87.3 %copy-start.2 = (s32[1,16,16]{2,1,0:T(8,128)S(1)}, s32[1,16,16]{2,1,0:T(8,128)}, u32[]{:S(2)}) copy-start(s32[1,16,16]{2,1,0:T(8,128)} %param.11) | copy-start | bytes 3076
  78.1 23.6 %all-to-all-start = ((bf16[64,16,256]{2,0,1:T(8,128)(2,1)}), bf16[64,16,256]{2,0,1:T(8,128)(2,1)S(1)}, u32[]{:S(2)}, u32[]{:S(2)}) async-start(bf16[64,16,256]{2,0,1:T(8,128)(2,1)} %bitcast.43), calls=%async_computation | async-start | bytes 1048576 | tf_op jit(solution)/shard_map/all_to_all | solution.py:98
  101.8 6.5 %copy-start.1 = (bf16[4096]{0:T(1024)(128)(2,1)S(1)}, bf16[4096]{0:T(1024)(128)(2,1)}, u32[]{:S(2)}) copy-start(bf16[4096]{0:T(1024)(128)(2,1)} %param.10) | copy-start | bytes 24580
  104.4 51.8 %all-to-all-start.1 = ((bf16[16,128,256]{1,2,0:T(8,128)(2,1)}), bf16[16,128,256]{1,2,0:T(8,128)(2,1)S(1)}, u32[]{:S(2)}, u32[]{:S(2)}) async-start(bf16[16,128,256]{1,2,0:T(8,128)(2,1)} %copy.37), calls=%async_computation.1 | async-start | bytes 2097152 | tf_op jit(solution)/shard_map/all_to_all | solution.py:103
where the time goes:
time: 159 us; the launch traced here: 158 us
  blocking collectives  47.1 us (30%)
  other arithmetic  45.5 us (29%)
  local copies, waits for them, and re-layouts  21 us (13%)
  matrix products  16.3 us (10%)
  waiting for transfers between devices  15.4 us (10%)
  starting transfers between devices  12.2 us (8%)
    unnamed x1, blocking collectives  44.8 us
    reduce_sum x4, other arithmetic, one_group(): jnp.einsum('dcph,dpl->dhl', left, low_onehot, preferred_element_type=jnp....  31.4 us
    all_to_all x1, waiting for transfers between devices, body(): lax.all_to_all(pair_cells, 'bits', split_axis=1, concat_axis=0, tiled=True)  15.4 us
    dot_general x4, matrix products, one_group(): jnp.einsum('dcph,dpl->dhl', left, low_onehot, preferred_element_type=jnp....  14.9 us
    reshape x2, local copies, waits for them, and re-layouts, build_filter(): jnp.broadcast_to(element_weights[:, :, None], (doc_count, elem_count, HAS...  12.4 us
    convert_element_type x4, other arithmetic, one_group(): (high_block[:, :, None] == jnp.arange(high_cells, dtype=jnp.int32)).astyp...  12.2 us
    all_to_all x1, starting transfers between devices, body(): lax.all_to_all(pair_cells, 'bits', split_axis=1, concat_axis=0, tiled=True)  8.26 us
    all_to_all x1, starting transfers between devices, body(): lax.all_to_all(picked_cells, 'bits', split_axis=0, concat_axis=2, tiled=T...  3.94 us
  transfers between devices with their start and end apart: 2, of which 1 were waited for; matrix products, arithmetic and copies ran while one was open for 2% of the time, Pallas kernels for 0%

commit v1 on v0

--- a/solution.py
+++ b/solution.py
@@ -95,7 +95,12 @@
         lax.all_gather(set_sizes.astype(jnp.float32), ("bits", "docs"), axis=0, tiled=True),
     )
     pair_cells = lax.all_gather(own_cells, "docs", axis=0, tiled=True)
-    slice_cells = lax.all_to_all(pair_cells, "bits", split_axis=1, concat_axis=0, tiled=True)
+    slice_cells = jnp.concatenate(
+        lax.all_to_all(
+            jnp.stack(jnp.split(pair_cells, lax.axis_size("bits"), axis=1)), "bits", 0, 0
+        ),
+        axis=0,
+    )
     tile_rows = row_group * row_half + (candidates[0][:, :, None] * TILE + tile_offsets).reshape(
         blocks, slot_count
     )

time: 159 us -> 168 us (1.057)
  local copies, waits for them, and re-layouts: 21 us -> 29.9 us
    unnamed x12 -> x27, local copies, waits for them, and re-layouts: 1.3 us -> 10.4 us
where the time goes in v1:
time: 168 us; the launch traced here: 167 us
  blocking collectives  47.1 us (28%)
  other arithmetic  45.5 us (27%)
  local copies, waits for them, and re-layouts  29.9 us (18%)
  matrix products  16.3 us (10%)
  waiting for transfers between devices  15.4 us (9%)
  starting transfers between devices  12.2 us (7%)
    unnamed x1, blocking collectives  44.8 us
    reduce_sum x4, other arithmetic, one_group(): jnp.einsum('dcph,dpl->dhl', left, low_onehot, preferred_element_type=jnp....  31.4 us
    all_to_all x1, waiting for transfers between devices, body(): lax.all_to_all(jnp.stack(jnp.split(pair_cells, lax.axis_size('bits'), axi...  15.4 us
    dot_general x4, matrix products, one_group(): jnp.einsum('dcph,dpl->dhl', left, low_onehot, preferred_element_type=jnp....  14.9 us
    reshape x2, local copies, waits for them, and re-layouts, build_filter(): jnp.broadcast_to(element_weights[:, :, None], (doc_count, elem_count, HAS...  12.4 us
    convert_element_type x4, other arithmetic, one_group(): (high_block[:, :, None] == jnp.arange(high_cells, dtype=jnp.int32)).astyp...  12.2 us
    unnamed x27, local copies, waits for them, and re-layouts  10.4 us
    all_to_all x1, starting transfers between devices, body(): lax.all_to_all(jnp.stack(jnp.split(pair_cells, lax.axis_size('bits'), axi...  8.26 us
  transfers between devices with their start and end apart: 2, of which 1 were waited for; matrix products, arithmetic and copies ran while one was open for 2% of the time, Pallas kernels for 0%

profile of v1, /device:TPU:0, one launch (start us, length us, event | category | flops | bytes accessed | tf_op | source)
XLA Modules:
  0.0 166.8 jit_solution(14337301838698218462)
XLA Ops:
  0.0 1.1 copy.28
  1.1 0.4 broadcast_in_dim.12
  1.5 5.7 %reshape.168 = f32[4,8,1,4096]{1,0,3,2:T(4,128)} reshape(f32[32,1024,4]{0,2,1:T(4,128)S(1)} %broadcast_in_dim.12) | data formatting | bytes 1048576 | tf_op jit(solution)/shard_map/reshape | solution.py:19
  7.2 6.7 %copy.29 = f32[4,8,1,4096]{3,1,2,0:T(8,128)S(1)} copy(f32[4,8,1,4096]{1,0,3,2:T(4,128)} %reshape.168) | data formatting | bytes 1048576 | tf_op jit(solution)/shard_map/reshape | solution.py:19
  14.3 0.3 subtract_bitcast_fusion
  14.7 60.3 %while.10 = (s32[]{:T(128)}, bf16[4,8,4096]{2,1,0:T(8,128)(2,1)S(1)}, bf16[4,8,3,4096]{3,1,2,0:T(8,128)(2,1)S(1)}, s32[4,8,4096]{2,1,0:T(8,128)S(1)}, s32[4,8,4096]{2,1,0:T(8,128)S(1)}, /*index=5*/s32[]{:T(128)}) while((s32[]{:T(128)}, bf16[4,8,4096]{2,1,0:T(8,128)(2,1)S(1)}, bf16[4,8,3,4096]{3,1,2,0:T(8,128)(2,1)S(1)}, ...), condition=%wide.region_2.3_spmd, body=%wide.region_0.2_spmd.sunk | while | flops 304087040 | bytes 18874448 | solution.py:44
  14.8 3.0 %fusion.39 = bf16[8,4096,64]{1,2,0:T(8,128)(2,1)} fusion(s32[8,4096]{1,0:T(8,128)S(1)} %get-tuple-element.109), kind=kLoop, calls=%fused_computation.5.clone.1 | loop fusion | flops 4194304 | bytes 4325376 | tf_op jit(solution)/shard_map/while/body/eval_jaxpr/convert_element_type | solution.py:34
  18.0 7.9 %convert_reduce_fusion.2 = bf16[8,4096,64]{1,2,0:T(8,128)(2,1)} fusion(bf16[8,4096,64]{1,2,0:T(8,128)(2,1)} %fusion.39, bf16[8,3,4096]{2,1,0:T(4,128)(2,1)S(1)} %bitcast.109), kind=kLoop, calls=%fused_computation.2.clone.1 | loop fusion | flops 29360128 | bytes 8585216 | tf_op jit(solution)/shard_map/while/body/eval_jaxpr/dcph,dpl->dhl/reduce_sum | solution.py:41
  25.9 3.7 %fusion.40 = bf16[8,64,64]{2,1,0:T(8,128)(2,1)S(1)} fusion(bf16[8,4096,64]{1,2,0:T(8,128)(2,1)} %convert_reduce_fusion.2, s32[8,4096]{1,0:T(8,128)S(1)} %get-tuple-element.110), kind=kOutput, calls=%fused_computation.6.clone.1 | convolution fusion | flops 270532608 | bytes 4390912 | tf_op jit(solution)/shard_map/while/body/eval_jaxpr/dcph,dpl->dhl/dot_general | solution.py:41
  29.8 3.0 %fusion.39 = bf16[8,4096,64]{1,2,0:T(8,128)(2,1)} fusion(s32[8,4096]{1,0:T(8,128)S(1)} %get-tuple-element.109), kind=kLoop, calls=%fused_computation.5.clone.1 | loop fusion | flops 4194304 | bytes 4325376 | tf_op jit(solution)/shard_map/while/body/eval_jaxpr/convert_element_type | solution.py:34
  33.1 7.9 %convert_reduce_fusion.2 = bf16[8,4096,64]{1,2,0:T(8,128)(2,1)} fusion(bf16[8,4096,64]{1,2,0:T(8,128)(2,1)} %fusion.39, bf16[8,3,4096]{2,1,0:T(4,128)(2,1)S(1)} %bitcast.109), kind=kLoop, calls=%fused_computation.2.clone.1 | loop fusion | flops 29360128 | bytes 8585216 | tf_op jit(solution)/shard_map/while/body/eval_jaxpr/dcph,dpl->dhl/reduce_sum | solution.py:41
  40.9 3.7 %fusion.40 = bf16[8,64,64]{2,1,0:T(8,128)(2,1)S(1)} fusion(bf16[8,4096,64]{1,2,0:T(8,128)(2,1)} %convert_reduce_fusion.2, s32[8,4096]{1,0:T(8,128)S(1)} %get-tuple-element.110), kind=kOutput, calls=%fused_computation.6.clone.1 | convolution fusion | flops 270532608 | bytes 4390912 | tf_op jit(solution)/shard_map/while/body/eval_jaxpr/dcph,dpl->dhl/dot_general | solution.py:41
  44.9 3.0 %fusion.39 = bf16[8,4096,64]{1,2,0:T(8,128)(2,1)} fusion(s32[8,4096]{1,0:T(8,128)S(1)} %get-tuple-element.109), kind=kLoop, calls=%fused_computation.5.clone.1 | loop fusion | flops 4194304 | bytes 4325376 | tf_op jit(solution)/shard_map/while/body/eval_jaxpr/convert_element_type | solution.py:34
  48.1 7.9 %convert_reduce_fusion.2 = bf16[8,4096,64]{1,2,0:T(8,128)(2,1)} fusion(bf16[8,4096,64]{1,2,0:T(8,128)(2,1)} %fusion.39, bf16[8,3,4096]{2,1,0:T(4,128)(2,1)S(1)} %bitcast.109), kind=kLoop, calls=%fused_computation.2.clone.1 | loop fusion | flops 29360128 | bytes 8585216 | tf_op jit(solution)/shard_map/while/body/eval_jaxpr/dcph,dpl->dhl/reduce_sum | solution.py:41
  56.0 3.7 %fusion.40 = bf16[8,64,64]{2,1,0:T(8,128)(2,1)S(1)} fusion(bf16[8,4096,64]{1,2,0:T(8,128)(2,1)} %convert_reduce_fusion.2, s32[8,4096]{1,0:T(8,128)S(1)} %get-tuple-element.110), kind=kOutput, calls=%fused_computation.6.clone.1 | convolution fusion | flops 270532608 | bytes 4390912 | tf_op jit(solution)/shard_map/while/body/eval_jaxpr/dcph,dpl->dhl/dot_general | solution.py:41
  60.0 3.0 %fusion.39 = bf16[8,4096,64]{1,2,0:T(8,128)(2,1)} fusion(s32[8,4096]{1,0:T(8,128)S(1)} %get-tuple-element.109), kind=kLoop, calls=%fused_computation.5.clone.1 | loop fusion | flops 4194304 | bytes 4325376 | tf_op jit(solution)/shard_map/while/body/eval_jaxpr/convert_element_type | solution.py:34
  63.2 7.9 %convert_reduce_fusion.2 = bf16[8,4096,64]{1,2,0:T(8,128)(2,1)} fusion(bf16[8,4096,64]{1,2,0:T(8,128)(2,1)} %fusion.39, bf16[8,3,4096]{2,1,0:T(4,128)(2,1)S(1)} %bitcast.109), kind=kLoop, calls=%fused_computation.2.clone.1 | loop fusion | flops 29360128 | bytes 8585216 | tf_op jit(solution)/shard_map/while/body/eval_jaxpr/dcph,dpl->dhl/reduce_sum | solution.py:41
  71.1 3.7 %fusion.40 = bf16[8,64,64]{2,1,0:T(8,128)(2,1)S(1)} fusion(bf16[8,4096,64]{1,2,0:T(8,128)(2,1)} %convert_reduce_fusion.2, s32[8,4096]{1,0:T(8,128)S(1)} %get-tuple-element.110), kind=kOutput, calls=%fused_computation.6.clone.1 | convolution fusion | flops 270532608 | bytes 4390912 | tf_op jit(solution)/shard_map/while/body/eval_jaxpr/dcph,dpl->dhl/dot_general | solution.py:41
  75.0 2.3 %all_gather.9 = bf16[64,4096]{1,0:T(8,128)(2,1)S(1)} all-gather(bf16[32,4096]{1,0:T(8,128)(2,1)S(1)} %bitcast.110), channel_id=1, replica_groups=mesh['bits'=16,'docs'=2] {'docs'}, dimensions={0}, use_global_device_ids=true | all-gather | bytes 786432 | tf_op jit(solution)/shard_map/all_gather | solution.py:97
  77.3 0.6 fusion.29
  77.9 0.6 fusion.28
  78.5 0.6 fusion.27
  79.1 0.6 fusion.26
  79.7 0.6 fusion.25
  80.3 0.6 fusion.24
  81.0 0.6 fusion.23
  81.6 0.6 fusion.22
  82.2 0.6 fusion.21
  82.8 0.6 fusion.20
  83.4 0.6 fusion.19
  84.0 0.6 fusion.18
  84.6 0.6 fusion.17
  85.2 0.6 fusion.16
  85.8 0.6 fusion.15
  86.4 0.6 fusion.14
  87.0 8.3 %all-to-all-start = ((bf16[16,64,256]{2,1,0:T(8,128)(2,1)}), bf16[16,64,256]{2,1,0:T(8,128)(2,1)S(1)}, u32[]{:S(2)}, u32[]{:S(2)}) async-start(bf16[16,64,256]{2,1,0:T(8,128)(2,1)} %fusion.14), calls=%async_computation | async-start | bytes 1048576 | tf_op jit(solution)/shard_map/all_to_all | solution.py:99
  95.3 15.4 %all-to-all-done = bf16[16,64,256]{2,1,0:T(8,128)(2,1)S(1)} async-done(((bf16[16,64,256]{2,1,0:T(8,128)(2,1)}), bf16[16,64,256]{2,1,0:T(8,128)(2,1)S(1)}, u32[]{:S(2)}, u32[]{:S(2)}) %all-to-all-start) | async-done | bytes 524320 | tf_op jit(solution)/shard_map/all_to_all | solution.py:99
  110.7 0.2 reshape_reshape.3
  110.9 0.5 convolution_convert_fusion
  111.4 0.5 reshape.171
  111.9 1.3 copy.31
  113.3 3.9 %all-to-all-start.1 = ((bf16[16,128,256]{1,2,0:T(8,128)(2,1)}), bf16[16,128,256]{1,2,0:T(8,128)(2,1)S(1)}, u32[]{:S(2)}, u32[]{:S(2)}) async-start(bf16[16,128,256]{1,2,0:T(8,128)(2,1)} %copy.31), calls=%async_computation.1 | async-start | bytes 2097152 | tf_op jit(solution)/shard_map/all_to_all | solution.py:108
  117.5 0.2 dynamic-update-slice
  117.8 44.8 %all-reduce.2 = (f32[1024]{0:T(1024)S(1)}, f32[1024]{0:T(1024)S(1)}) all-reduce(f32[1024]{0:T(1024)S(1)} %convert_dynamic-update-slice_fusion, f32[1024]{0:T(1024)S(1)} %dynamic-update-slice), channel_id=1, replica_groups=mesh['bits'=16,'docs'=2] {'bits','docs'}, use_global_device_ids=true, to_apply=%add.1 | all-reduce | flops 2048 | bytes 16384
  163.1 1.0 gather_fusion
  164.1 1.0 gather_fusion.1
  165.1 0.8 bitcast_multiply_fusion
  165.9 1.0 divide_bitcast_fusion
  (50 shorter events, 2.9 us)
Async XLA Ops:
  7.2 6.7 %copy-start.3 = (s32[32]{0:T(128)S(1)}, s32[32]{0:T(128)}, u32[]{:S(2)}) copy-start(s32[32]{0:T(128)} %param.9) | copy-start | bytes 388
  7.2 7.1 %copy-start = (s32[32,4096]{1,0:T(8,128)S(1)}, s32[32,4096]{1,0:T(8,128)}, u32[]{:S(2)}) copy-start(s32[32,4096]{1,0:T(8,128)} %param.7) | copy-start | bytes 1572868
  14.7 96.2 %copy-start.2 = (s32[1,16,16]{2,1,0:T(8,128)S(1)}, s32[1,16,16]{2,1,0:T(8,128)}, u32[]{:S(2)}) copy-start(s32[1,16,16]{2,1,0:T(8,128)} %param.11) | copy-start | bytes 3076
  87.0 23.6 %all-to-all-start = ((bf16[16,64,256]{2,1,0:T(8,128)(2,1)}), bf16[16,64,256]{2,1,0:T(8,128)(2,1)S(1)}, u32[]{:S(2)}, u32[]{:S(2)}) async-start(bf16[16,64,256]{2,1,0:T(8,128)(2,1)} %fusion.14), calls=%async_computation | async-start | bytes 1048576 | tf_op jit(solution)/shard_map/all_to_all | solution.py:99
  95.3 21.9 %copy-start.1 = (bf16[4096]{0:T(1024)(128)(2,1)S(1)}, bf16[4096]{0:T(1024)(128)(2,1)}, u32[]{:S(2)}) copy-start(bf16[4096]{0:T(1024)(128)(2,1)} %param.10) | copy-start | bytes 24580
  113.3 51.8 %all-to-all-start.1 = ((bf16[16,128,256]{1,2,0:T(8,128)(2,1)}), bf16[16,128,256]{1,2,0:T(8,128)(2,1)S(1)}, u32[]{:S(2)}, u32[]{:S(2)}) async-start(bf16[16,128,256]{1,2,0:T(8,128)(2,1)} %copy.31), calls=%async_computation.1 | async-start | bytes 2097152 | tf_op jit(solution)/shard_map/all_to_all | solution.py:108
